TPU v7x, 128 devices: a whole 4x4x4 slice. The times are simulated.
128 devices in a mesh: lat: 32 (over z, x, core), lev: 4 (over y).
Axes of the slice: x: 4, y: 4, z: 4, core: 2. Of those that a mesh axis runs over, the one named last changes fastest.
Arguments:
- grid: bfloat16 [640, 128, 4, 1280], P('lat', 'lev'), may hold values from -6 to 6
- legendre: bfloat16 [640, 640, 640], P('lat'), may hold values from -0.25 to 0.25
- vertical: bfloat16 [128, 128], P('lev'), may hold values from -0.5 to 0.5
- damping: bfloat16 [128], P('lev'), may hold values from 1 to 16
- lon_counts: int32 [640], replicated, may hold values from 160 to 1280
- wave_slots: int32 [640], replicated, may hold values from 0 to 639, as said below
Outputs:
- filtered_grid: bfloat16 [640, 128, 4, 1280], P('lat', 'lev')
Inputs may be any that keep to these rules, and one draw needn't show every extreme that they name: wave_slots is a permutation; slot g * 5 + r holds a wavenumber from r * 128 to (r + 1) * 128 - 1.
All inputs are finite; a program needn't handle non-finite values.
Results may differ from a plain program's by a relative error of at most 0.0074.
Values may be sent and summed in bfloat16 or wider, within the bound.
A program may use at most 128 MiB of HBM per device.

v0:
```python
import math
import jax
import jax.numpy as jnp
from jax import lax
from jax.sharding import PartitionSpec as P


def sent_together(arrays, axis, dim, along):
    widths = [math.prod(a.shape[along:]) for a in arrays]
    both = jnp.concatenate(
        [a.reshape(*a.shape[:along], w) for a, w in zip(arrays, widths)], axis=along
    )
    result = lax.all_gather(both, axis, axis=dim, tiled=True)
    pieces = jnp.split(result, [sum(widths[:k]) for k in range(1, len(widths))], axis=along)
    return tuple(
        (b.reshape(*result.shape[:along], *a.shape[along:]) for a, b in zip(arrays, pieces))
    )


def in_blocks(array, dim, peers):
    before, after = (array.shape[:dim], array.shape[dim + 1 :])
    return jnp.moveaxis(array.reshape(*before, peers, -1, *after), dim, 0)


def in_order(pieces, dim):
    lengths = list(pieces.shape[1:])
    lengths[dim] *= pieces.shape[0]
    return jnp.moveaxis(pieces, 0, dim).reshape(lengths)


def joined_exchange(array, axis, axes, splits, concats):
    sizes = [lax.axis_size(a) for a in axes]
    pieces = in_blocks(array, splits[0], sizes[0])
    pieces = jnp.moveaxis(in_blocks(pieces, splits[1] + 1, sizes[1]), 0, 1)
    inside = pieces.shape[2:]
    pieces = pieces.reshape(-1, *inside)
    pieces = lax.all_to_all(pieces, axis, split_axis=0, concat_axis=0, tiled=True)
    pieces = in_order(pieces.reshape(*sizes, *inside), concats[0] + 1)
    return in_order(pieces, concats[1])


def forward_build(wavenumbers, longitudes):
    points = jnp.arange(longitudes, dtype=jnp.int32)
    phase = (wavenumbers[:, None] * points[None, :] % longitudes).astype(jnp.float32) * (
        2.0 * math.pi / longitudes
    )
    scale = 1.0 / math.sqrt(longitudes)
    return jnp.stack([jnp.cos(phase) * scale, -jnp.sin(phase) * scale], axis=1).astype(jnp.bfloat16)


def inverse_build(wavenumbers, longitudes):
    points = jnp.arange(longitudes, dtype=jnp.int32)
    phase = (wavenumbers[:, None] * points[None, :] % longitudes).astype(jnp.float32) * (
        2.0 * math.pi / longitudes
    )
    scale = 1.0 / math.sqrt(longitudes)
    weight = jnp.where(wavenumbers == 0, 1.0, 2.0).astype(jnp.float32)[:, None]
    return jnp.stack(
        [jnp.cos(phase) * scale * weight, -jnp.sin(phase) * scale * weight], axis=1
    ).astype(jnp.bfloat16)


def damping_factor(degrees, damping):
    degree_values = jnp.arange(degrees).astype(jnp.float32)
    ratio = degree_values * (degree_values + 1.0) / float(degrees * (degrees - 1))
    return 1.0 / (1.0 + damping.astype(jnp.float32)[None, :] * (ratio * ratio)[:, None])


def legendre_forward(table, fourier, wavenumbers):
    degrees = table.shape[1]
    spectral = jnp.einsum("sna,srac->snrc", table, fourier, preferred_element_type=jnp.float32)
    live = (jnp.arange(degrees, dtype=jnp.int32)[None, :] >= wavenumbers[:, None]).astype(
        jnp.float32
    )
    return (spectral * live[:, :, None, None]).astype(jnp.bfloat16)


def legendre_inverse(table, mixed):
    banded = jnp.einsum("sna,snrc->srac", table, mixed, preferred_element_type=jnp.float32)
    return banded.astype(jnp.bfloat16)


def per_device(grid, legendre, vertical, damping, lon_counts, wave_slots):
    lat_rows, level_rows, fields, longitudes = grid.shape
    slot_count = wave_slots.shape[0]
    degrees = legendre.shape[1]
    own_slots = legendre.shape[0]
    forward_table = forward_build(wave_slots, longitudes)
    own_counts = lax.dynamic_slice_in_dim(lon_counts, lax.axis_index("lat") * lat_rows, lat_rows)
    fourier = jnp.einsum("mrx,alfx->mralf", forward_table, grid, preferred_element_type=jnp.float32)
    fourier = fourier.reshape(slot_count, 2, lat_rows, level_rows * fields)
    forward_kept = (2 * wave_slots[:, None] < own_counts[None, :]).astype(jnp.float32)
    fourier = (fourier * forward_kept[:, None, :, None]).astype(jnp.bfloat16)
    gathered = lax.all_to_all(
        lax.all_to_all(fourier, "lat", split_axis=0, concat_axis=2, tiled=True),
        "lev",
        split_axis=0,
        concat_axis=3,
        tiled=True,
    )
    count = gathered.shape[0]
    own_table = lax.dynamic_slice_in_dim(legendre, lax.axis_index("lev") * count, count, 0)
    own_waves = lax.dynamic_slice_in_dim(
        wave_slots, lax.axis_index("lat") * own_slots + lax.axis_index("lev") * count, count
    )
    spectral = legendre_forward(own_table, gathered, own_waves)
    all_rows, all_damping = sent_together((vertical, damping), "lev", 0, 1)
    levels = all_rows.shape[0]
    stacked = spectral.reshape(count, degrees, 2, levels, fields)
    mixed = stacked.astype(jnp.float32) + jnp.einsum(
        "snrkf,lk->snrlf", stacked, all_rows, preferred_element_type=jnp.float32
    )
    mixed = mixed * damping_factor(degrees, all_damping)[None, :, None, :, None]
    mixed = mixed.astype(jnp.bfloat16).reshape(count, degrees, 2, levels * fields)
    banded = legendre_inverse(own_table, mixed)
    returned = joined_exchange(banded, ("lat", "lev"), ("lat", "lev"), (2, 3), (0, 0))
    back_order = (
        wave_slots.reshape(lax.axis_size("lat"), lax.axis_size("lev"), count)
        .transpose(1, 0, 2)
        .reshape(slot_count)
    )
    inverse_table = inverse_build(back_order, longitudes)
    back_kept = (2 * back_order[:, None] < own_counts[None, :]).astype(jnp.bfloat16)
    returned = returned * back_kept[:, None, :, None]
    filtered_grid = jnp.einsum(
        "mrac,mrx->acx", returned, inverse_table, preferred_element_type=jnp.float32
    )
    return filtered_grid.reshape(lat_rows, level_rows, fields, longitudes).astype(jnp.bfloat16)


def solution(mesh):
    return jax.shard_map(
        per_device,
        mesh=mesh,
        in_specs=(
            P("lat", "lev", None, None),
            P("lat", None, None),
            P("lev", None),
            P("lev"),
            P(),
            P(),
        ),
        out_specs=P("lat", "lev", None, None),
        check_vma=False,
    )
```

profile of v0, /device:TPU:3, one launch (start us, length us, event | category | flops | bytes accessed | tf_op | source)
XLA Modules:
  0.0 534.7 jit_solution(11057568427985806592)
XLA Ops:
  0.0 15.9 %multiply_convert_fusion.5 = (bf16[640,1,1280]{2,0,1:T(8,128)(2,1)S(1)}, bf16[640,1,1280]{2,0,1:T(8,128)(2,1)S(1)}) fusion(s32[640]{0:T(1024)} %param.11), kind=kLoop, calls=%fused_computation.38 | loop fusion | flops 11468800 | bytes 3279360 | tf_op jit(solution)/shard_map/convert.3
  16.9 12.1 %fusion.2 = f32[640,2,20,32,4]{0,3,4,2,1:T(8,128)S(1)} fusion(bf16[20,32,4,1280]{3,2,1,0:T(4,128)(2,1)} %param.6, bf16[640,1,1280]{2,0,1:T(8,128)(2,1)S(1)} %get-tuple-element.12, bf16[640,1,1280]{2,0,1:T(8,128)(2,1)S(1)} %get-tuple-element.11), kind=kOutput, calls=%fused_computation.8 | convolution fusion | flops 8395161600 | bytes 22937600 | tf_op jit(solution)/shard_map/mrx,alfx->mralf/dot_general | solution.py:90
  29.0 15.4 %copy.70 = f32[640,2,20,32,4]{0,1,4,3,2:T(2,128)} copy(f32[640,2,20,32,4]{0,3,4,2,1:T(8,128)S(1)} %fusion.2) | data formatting | bytes 26214400 | tf_op jit(solution)/shard_map/mrx,alfx->mralf/dot_general | solution.py:90
  45.5 7.9 %multiply_convert_fusion.1 = bf16[640,2,20,128]{0,1,3,2:T(2,128)(2,1)} fusion(f32[640,2,20,128]{0,1,3,2:T(2,128)} %bitcast.64, f32[640,20]{0,1:T(8,128)S(1)} %get-tuple-element.14), kind=kLoop, calls=%fused_computation.5 | loop fusion | flops 6553600 | bytes 19712000 | tf_op jit(solution)/shard_map/convert_element_type | solution.py:93
  53.5 22.8 %copy.71 = bf16[640,2,20,128]{3,1,2,0:T(2,128)(2,1)} copy(bf16[640,2,20,128]{0,1,3,2:T(2,128)(2,1)} %multiply_convert_fusion.1) | data formatting | bytes 13107200 | tf_op jit(solution)/shard_map/convert_element_type | solution.py:93
  76.3 84.1 %all_to_all.41 = bf16[640,2,20,128]{3,1,2,0:T(2,128)(2,1)S(1)} all-to-all(bf16[640,2,20,128]{3,1,2,0:T(2,128)(2,1)} %copy.71), channel_id=1, replica_groups=mesh['lat'=32,'lev'=4] {'lat'}, dimensions={0} | all-to-all | bytes 13107200 | tf_op jit(solution)/shard_map/all_to_all | solution.py:95
  171.9 77.4 %all_gather.3 = bf16[128,129]{1,0:T(8,128)(2,1)S(1)} all-gather(bf16[32,129]{1,0:T(8,128)(2,1)S(1)} %pad_maximum_fusion.1), channel_id=1, replica_groups=mesh['lat'=32,'lev'=4] {'lev'}, dimensions={0}, use_global_device_ids=true | all-gather | bytes 41280 | tf_op jit(solution)/shard_map/all_gather | solution.py:13
  249.6 7.2 %copy.73 = bf16[20,2,640,128]{3,2,1,0:T(8,128)(2,1)} copy(bf16[20,2,640,128]{3,1,2,0:T(2,128)(2,1)} %all-to-all-done.1) | data formatting | bytes 13107200 | tf_op jit(solution)/shard_map/all_to_all | solution.py:94
  256.8 9.5 %copy.74 = bf16[5,2,640,4,128]{2,4,3,1,0:T(8,128)(2,1)} copy(bf16[5,2,640,4,128]{4,2,1,0,3:T(8,128)(2,1)} %bitcast.70) | data formatting | bytes 13107200 | tf_op jit(solution)/shard_map/all_to_all | solution.py:94
  266.3 11.1 %multiply_convert_fusion = bf16[5,640,2,512]{1,3,2,0:T(8,128)(2,1)} fusion(bf16[5,2,640,512]{2,3,1,0:T(8,128)(2,1)} %bitcast.72, f32[5,640]{1,0:T(8,128)S(1)} %fusion.29, bf16[20,640,640]{2,1,0:T(8,128)(2,1)} %param.7, s32[]{:T(128)S(6)} %select_n.50), kind=kOutput, calls=%fused_computation.4 | convolution fusion | flops 4200857600 | bytes 17216004 | tf_op jit(solution)/shard_map/sna,srac->snrc/dot_general | solution.py:71
  277.4 11.8 %reshape.389 = bf16[5,640,2,128,4]{1,4,3,2,0:T(4,128)(2,1)} reshape(bf16[5,640,2,512]{1,3,2,0:T(8,128)(2,1)} %multiply_convert_fusion) | data formatting | bytes 13107200 | tf_op jit(solution)/shard_map/reshape | solution.py:109
  289.2 7.9 %fusion.1 = bf16[5,640,2,128,4]{1,3,4,2,0:T(8,128)(2,1)S(1)} fusion(bf16[5,640,2,128,4]{1,4,3,2,0:T(4,128)(2,1)} %reshape.389, f32[640,128]{0,1:T(8,128)S(1)} %add_divide_fusion, bf16[128,129]{1,0:T(8,128)(2,1)S(1)} %all_gather.3), kind=kOutput, calls=%fused_computation.3 | convolution fusion | flops 851968000 | bytes 20021248 | tf_op jit(solution)/shard_map/snrkf,lk->snrlf/dot_general | solution.py:110
  297.1 28.2 %copy.78 = bf16[5,640,2,128,4]{1,2,4,3,0:T(2,128)(2,1)S(1)} copy(bf16[5,640,2,128,4]{1,3,4,2,0:T(8,128)(2,1)S(1)} %fusion.1) | data formatting | bytes 13107200 | tf_op jit(solution)/shard_map/convert_element_type | solution.py:114
  325.3 10.1 %convert_bitcast_fusion = bf16[5,2,640,512]{2,3,1,0:T(8,128)(2,1)} fusion(bf16[5,640,2,512]{1,2,3,0:T(2,128)(2,1)S(1)} %bitcast.73, bf16[20,640,640]{2,1,0:T(8,128)(2,1)} %param.7, s32[]{:T(128)S(6)} %select_n.50), kind=kOutput, calls=%fused_computation.15 | convolution fusion | flops 4197580800 | bytes 17203204 | tf_op jit(solution)/shard_map/sna,snrc->srac/dot_general | solution.py:79
  335.4 16.7 %copy.80 = bf16[5,2,640,512]{3,1,2,0:T(2,128)(2,1)} copy(bf16[5,2,640,512]{2,3,1,0:T(8,128)(2,1)} %convert_bitcast_fusion) | data formatting | bytes 13107200 | tf_op jit(solution)/shard_map/convert_element_type | solution.py:80
  352.1 7.1 %fusion.36 = (bf16[32,5,2,20,128]{4,2,3,0,1:T(2,128)(2,1)S(1)}, bf16[32,5,2,20,128]{4,2,3,0,1:T(2,128)(2,1)S(1)}, bf16[32,5,2,20,128]{4,2,3,0,1:T(2,128)(2,1)S(1)}, bf16[32,5,2,20,128]{4,2,3,0,1:T(2,128)(2,1)S(1)}) fusion(bf16[32,5,2,20,512]{4,2,3,0,1:T(2,128)(2,1)} %bitcast.67), kind=kLoop, calls=%fused_computation.62 | loop fusion | bytes 13107200 | tf_op jit(solution)/shard_map/slice
  359.2 11.0 %pad_maximum_fusion = bf16[32,20,2,20,128]{4,2,3,0,1:T(2,128)(2,1)S(1)} fusion(bf16[32,5,2,20,128]{4,2,3,0,1:T(2,128)(2,1)S(1)} %get-tuple-element.6, bf16[32,5,2,20,128]{4,2,3,0,1:T(2,128)(2,1)S(1)} %get-tuple-element.7, bf16[32,5,2,20,128]{4,2,3,0,1:T(2,128)(2,1)S(1)} %get-tuple-element.8, bf16[32,5,2,20,128]{4,2,3,0,1:T(2,128)(2,1)S(1)} %get-tuple-element.5), kind=kLoop, calls=%fused_computation.6 | loop fusion | flops 9830400 | bytes 13107200 | tf_op jit(solution)/shard_map/concatenate
  376.0 8.1 %all-to-all-start.2 = ((bf16[128,5,2,20,128]{4,2,3,1,0:T(2,128)(2,1)}), bf16[128,5,2,20,128]{4,2,3,1,0:T(2,128)(2,1)}, u32[]{:S(2)}, u32[]{:S(2)}) async-start(bf16[128,5,2,20,128]{4,2,3,1,0:T(2,128)(2,1)} %bitcast.66), calls=%async_computation.2 | async-start | bytes 13107200 | tf_op jit(solution)/shard_map/all_to_all | solution.py:37
  384.4 15.2 %multiply_convert_fusion.3 = (bf16[640,1,1280]{2,0,1:T(8,128)(2,1)S(1)}, bf16[640,1,1280]{2,0,1:T(8,128)(2,1)S(1)}) fusion(f32[640]{0:T(1024)S(1)} %select_multiply_fusion, s32[640]{0:T(1024)S(1)} %broadcast_in_dim_reshape.4), kind=kLoop, calls=%fused_computation.33 | loop fusion | flops 11468800 | bytes 3281920 | tf_op jit(solution)/shard_map/convert.1
  399.5 63.9 %all-to-all-done.2 = bf16[128,5,2,20,128]{4,2,3,1,0:T(2,128)(2,1)} async-done(((bf16[128,5,2,20,128]{4,2,3,1,0:T(2,128)(2,1)}), bf16[128,5,2,20,128]{4,2,3,1,0:T(2,128)(2,1)}, u32[]{:S(2)}, u32[]{:S(2)}) %all-to-all-start.2) | async-done | bytes 6553632 | tf_op jit(solution)/shard_map/all_to_all | solution.py:37
  469.5 17.0 %bitcast_multiply_fusion = bf16[640,2,20,128]{3,1,2,0:T(2,128)(2,1)} fusion(bf16[32,4,5,2,20,128]{5,3,4,2,0,1:T(2,128)(2,1)S(1)} %copy.82, bf16[640,20]{1,0:T(8,128)(2,1)S(1)} %copy.84), kind=kLoop, calls=%fused_computation.7 | loop fusion | flops 3276800 | bytes 13132800 | tf_op jit(solution)/shard_map/mul | solution.py:124
  486.5 23.5 %copy.85 = bf16[20,128,640,2]{2,3,1,0:T(2,128)(2,1)} copy(bf16[20,128,640,2]{1,3,0,2:T(2,128)(2,1)} %bitcast.68) | data formatting | bytes 13107200 | tf_op jit(solution)/shard_map/mrac,mrx->acx/dot_general | solution.py:125
  510.0 13.3 %bitcast_convert_fusion = bf16[20,32,4,1280]{3,1,2,0:T(8,128)(2,1)} fusion(bf16[20,32,4,640,2]{3,4,2,1,0:T(2,128)(2,1)} %bitcast.71, bf16[640,1,1280]{2,0,1:T(8,128)(2,1)S(1)} %get-tuple-element.10, bf16[640,1,1280]{2,0,1:T(8,128)(2,1)S(1)} %get-tuple-element.9), kind=kOutput, calls=%fused_computation | convolution fusion | flops 8393523200 | bytes 16384000 | tf_op jit(solution)/shard_map/mrac,mrx->acx/dot_general | solution.py:125
  523.3 11.4 %copy.87 = bf16[20,32,4,1280]{3,2,1,0:T(4,128)(2,1)} copy(bf16[20,32,4,1280]{3,1,2,0:T(8,128)(2,1)} %bitcast_convert_fusion) | data formatting | bytes 13107200 | tf_op jit(solution)/shard_map/convert_element_type | solution.py:128
  (26 shorter events, 25.8 us)
Async XLA Ops:
  29.0 15.6 %copy-start = (s32[640]{0:T(1024)S(1)}, s32[640]{0:T(1024)}, u32[]{:S(2)}) copy-start(s32[640]{0:T(1024)} %param.11) | copy-start | bytes 7684
  166.3 5.5 %copy-start.2 = (bf16[32]{0:T(256)(128)(2,1)S(1)}, bf16[32]{0:T(256)(128)(2,1)}, u32[]{:S(2)}) copy-start(bf16[32]{0:T(256)(128)(2,1)} %param.9) | copy-start | bytes 196
  166.3 5.6 %copy-start.1 = (bf16[32,128]{1,0:T(8,128)(2,1)S(1)}, bf16[32,128]{1,0:T(8,128)(2,1)}, u32[]{:S(2)}) copy-start(bf16[32,128]{1,0:T(8,128)(2,1)} %param.8) | copy-start | bytes 24580
  166.3 83.3 %all-to-all-start.1 = ((bf16[20,2,640,128]{3,1,2,0:T(2,128)(2,1)}), bf16[20,2,640,128]{3,1,2,0:T(2,128)(2,1)}, u32[]{:S(2)}, u32[]{:S(2)}) async-start(bf16[20,2,640,128]{3,1,2,0:T(2,128)(2,1)} %bitcast.65), calls=%async_computation.1 | async-start | bytes 13107200 | tf_op jit(solution)/shard_map/all_to_all | solution.py:94
  376.0 87.4 %all-to-all-start.2 = ((bf16[128,5,2,20,128]{4,2,3,1,0:T(2,128)(2,1)}), bf16[128,5,2,20,128]{4,2,3,1,0:T(2,128)(2,1)}, u32[]{:S(2)}, u32[]{:S(2)}) async-start(bf16[128,5,2,20,128]{4,2,3,1,0:T(2,128)(2,1)} %bitcast.66), calls=%async_computation.2 | async-start | bytes 13107200 | tf_op jit(solution)/shard_map/all_to_all | solution.py:37
where the time goes:
time: 537 us; the launch traced here: 535 us
  local copies, waits for them, and re-layouts  174 us (32%)
  blocking collectives  162 us (30%)
  other arithmetic  67.4 us (13%)
  waiting for transfers between devices  63.9 us (12%)
  matrix products  54.5 us (10%)
  starting transfers between devices  13.6 us (3%)
    all_to_all x1, blocking collectives, per_device(): lax.all_to_all(fourier, 'lat', split_axis=0, concat_axis=2, tiled=True)  84.1 us
    all_gather x1, blocking collectives, sent_together(): result = lax.all_gather(both, axis, axis=dim, tiled=True)  77.4 us
    all_to_all x1, waiting for transfers between devices, joined_exchange(): lax.all_to_all(pieces, axis, split_axis=0, concat_axis=0, tiled=True)  63.9 us
    another operation x2, other arithmetic  31.1 us
    convert_element_type x1, local copies, waits for them, and re-layouts, per_device(): mixed.astype(jnp.bfloat16).reshape(count, degrees, 2, levels * fields)  28.2 us
    dot_general x1, local copies, waits for them, and re-layouts, per_device(): jnp.einsum('mrac,mrx->acx', returned, inverse_table, preferred_element_ty...  23.5 us
    convert_element_type x1, local copies, waits for them, and re-layouts, per_device(): fourier = (fourier * forward_kept[:, None, :, None]).astype(jnp.bfloat16)  22.8 us
    mul x1, other arithmetic, per_device(): returned = returned * back_kept[:, None, :, None]  17 us
  transfers between devices with their start and end apart: 2, of which 1 were waited for; matrix products, arithmetic and copies ran while one was open for 3% of the time, Pallas kernels for 0%

commit v1 on v0

--- a/solution.py
+++ b/solution.py
@@ -3,6 +3,18 @@
 import jax.numpy as jnp
 from jax import lax
 from jax.sharding import PartitionSpec as P
+
+
+def exchange_directly(array, axis, split, join):
+    ways, here = (lax.axis_size(axis), lax.axis_index(axis))
+    width = array.shape[split] // ways
+    turned = jnp.roll(array, -here * width, axis=split)
+    got = [lax.slice_in_dim(turned, 0, width, axis=split)]
+    for far in range(1, ways):
+        sent = lax.slice_in_dim(turned, far * width, (far + 1) * width, axis=split)
+        got.append(lax.ppermute(sent, axis, [(d, (d + far) % ways) for d in range(ways)]))
+    line = jnp.concatenate(got[::-1], axis=join)
+    return jnp.roll(line, (here + 1) * got[0].shape[join], axis=join)
 
 
 def sent_together(arrays, axis, dim, along):
@@ -91,12 +103,8 @@
     fourier = fourier.reshape(slot_count, 2, lat_rows, level_rows * fields)
     forward_kept = (2 * wave_slots[:, None] < own_counts[None, :]).astype(jnp.float32)
     fourier = (fourier * forward_kept[:, None, :, None]).astype(jnp.bfloat16)
-    gathered = lax.all_to_all(
-        lax.all_to_all(fourier, "lat", split_axis=0, concat_axis=2, tiled=True),
-        "lev",
-        split_axis=0,
-        concat_axis=3,
-        tiled=True,
+    gathered = exchange_directly(
+        lax.all_to_all(fourier, "lat", split_axis=0, concat_axis=2, tiled=True), "lev", 0, 3
     )
     count = gathered.shape[0]
     own_table = lax.dynamic_slice_in_dim(legendre, lax.axis_index("lev") * count, count, 0)

time: 537 us -> 582 us (1.084); the launches traced: 535 us -> 573 us
  blocking collectives: 162 us -> 77.5 us
  waiting for transfers between devices: 63.9 us -> 142 us
  local copies, waits for them, and re-layouts: 174 us -> 200 us
  other arithmetic: 67.4 us -> 76.4 us
  starting transfers between devices: 13.6 us -> 21.9 us
    all_to_all x1 -> x0, blocking collectives: 84.1 us -> none  [per_device(): lax.all_to_all(fourier, 'lat', split_axis=0, concat_axis=2, tiled=True)]
    all_to_all x1, waiting for transfers between devices: 0.01 us -> 78.1 us  [per_device(): lax.all_to_all(fourier, 'lat', split_axis=0, concat_axis=2, tiled=True)]
    unnamed x6 -> x15, local copies, waits for them, and re-layouts: 0.01 us -> 18.5 us
    all_to_all x1 -> x2, local copies, waits for them, and re-layouts: 5.81 us -> 23.6 us  [per_device(): lax.all_to_all(fourier, 'lat', split_axis=0, concat_axis=2, tiled=True)]
    all_to_all x2 -> x0, local copies, waits for them, and re-layouts: 16.7 us -> none  [per_device(): lax.all_to_all(lax.all_to_all(fourier, 'lat', split_axis=0, concat_axis=2...]
    another operation x2 -> x3, other arithmetic: 31.1 us -> 42.1 us
    another operation x0 -> x1, local copies, waits for them, and re-layouts: none -> 5.88 us
    slice x1 -> x2, local copies, waits for them, and re-layouts: 7.1 us -> 12 us
  transfers between devices with their start and end apart: 2 -> 5, of which waited for: 1 -> 2; matrix products, arithmetic and copies ran while one was open for 3% -> 4% of each run, Pallas kernels for 0% -> 0%
where the time goes in v1:
time: 582 us; the launch traced here: 573 us
  local copies, waits for them, and re-layouts  200 us (34%)
  waiting for transfers between devices  142 us (24%)
  blocking collectives  77.5 us (13%)
  other arithmetic  76.4 us (13%)
  matrix products  55.1 us (9%)
  starting transfers between devices  21.9 us (4%)
    all_to_all x1, waiting for transfers between devices, per_device(): lax.all_to_all(fourier, 'lat', split_axis=0, concat_axis=2, tiled=True)  78.1 us
    all_gather x1, blocking collectives, sent_together(): result = lax.all_gather(both, axis, axis=dim, tiled=True)  77.5 us
    all_to_all x1, waiting for transfers between devices, joined_exchange(): lax.all_to_all(pieces, axis, split_axis=0, concat_axis=0, tiled=True)  63.9 us
    another operation x3, other arithmetic  42.1 us
    convert_element_type x1, local copies, waits for them, and re-layouts, per_device(): mixed.astype(jnp.bfloat16).reshape(count, degrees, 2, levels * fields)  28.2 us
    all_to_all x2, local copies, waits for them, and re-layouts, per_device(): lax.all_to_all(fourier, 'lat', split_axis=0, concat_axis=2, tiled=True)  23.6 us
    dot_general x1, local copies, waits for them, and re-layouts, per_device(): jnp.einsum('mrac,mrx->acx', returned, inverse_table, preferred_element_ty...  23.5 us
    convert_element_type x1, local copies, waits for them, and re-layouts, per_device(): fourier = (fourier * forward_kept[:, None, :, None]).astype(jnp.bfloat16)  22.8 us
  transfers between devices with their start and end apart: 5, of which 2 were waited for; matrix products, arithmetic and copies ran while one was open for 4% of the time, Pallas kernels for 0%

profile of v1, /device:TPU:3, one launch (start us, length us, event | category | flops | bytes accessed | tf_op | source)
XLA Modules:
  0.0 573.5 jit_solution(1180536864654457044)
XLA Ops:
  0.9 15.9 %multiply_convert_fusion.5 = (bf16[640,1,1280]{2,0,1:T(8,128)(2,1)S(1)}, bf16[640,1,1280]{2,0,1:T(8,128)(2,1)S(1)}) fusion(s32[640]{0:T(1024)} %param.11), kind=kLoop, calls=%fused_computation.42 | loop fusion | flops 11468800 | bytes 3279360 | tf_op jit(solution)/shard_map/convert.3
  17.8 12.1 %fusion.3 = f32[640,2,20,32,4]{0,3,4,2,1:T(8,128)S(1)} fusion(bf16[20,32,4,1280]{3,2,1,0:T(4,128)(2,1)} %param.6, bf16[640,1,1280]{2,0,1:T(8,128)(2,1)S(1)} %get-tuple-element.15, bf16[640,1,1280]{2,0,1:T(8,128)(2,1)S(1)} %get-tuple-element.14), kind=kOutput, calls=%fused_computation.11 | convolution fusion | flops 8395161600 | bytes 22937600 | tf_op jit(solution)/shard_map/mrx,alfx->mralf/dot_general | solution.py:102
  29.9 15.4 %copy.52 = f32[640,2,20,32,4]{0,1,4,3,2:T(2,128)} copy(f32[640,2,20,32,4]{0,3,4,2,1:T(8,128)S(1)} %fusion.3) | data formatting | bytes 26214400 | tf_op jit(solution)/shard_map/mrx,alfx->mralf/dot_general | solution.py:102
  46.2 7.9 %multiply_convert_fusion.1 = bf16[640,2,20,128]{0,1,3,2:T(2,128)(2,1)} fusion(f32[640,2,20,128]{0,1,3,2:T(2,128)} %bitcast.59, f32[640,20]{0,1:T(8,128)S(1)} %get-tuple-element.17), kind=kLoop, calls=%fused_computation.7 | loop fusion | flops 6553600 | bytes 19712000 | tf_op jit(solution)/shard_map/convert_element_type | solution.py:105
  54.1 22.8 %copy.53 = bf16[640,2,20,128]{3,1,2,0:T(2,128)(2,1)} copy(bf16[640,2,20,128]{0,1,3,2:T(2,128)(2,1)} %multiply_convert_fusion.1) | data formatting | bytes 13107200 | tf_op jit(solution)/shard_map/convert_element_type | solution.py:105
  77.0 9.3 %all-to-all-start = ((bf16[640,2,20,128]{3,1,2,0:T(2,128)(2,1)}), bf16[640,2,20,128]{3,1,2,0:T(2,128)(2,1)}, u32[]{:S(2)}, u32[]{:S(2)}) async-start(bf16[640,2,20,128]{3,1,2,0:T(2,128)(2,1)} %copy.53), calls=%async_computation | async-start | bytes 13107200 | tf_op jit(solution)/shard_map/all_to_all | solution.py:107
  86.3 78.1 %all-to-all-done = bf16[640,2,20,128]{3,1,2,0:T(2,128)(2,1)} async-done(((bf16[640,2,20,128]{3,1,2,0:T(2,128)(2,1)}), bf16[640,2,20,128]{3,1,2,0:T(2,128)(2,1)}, u32[]{:S(2)}, u32[]{:S(2)}) %all-to-all-start) | async-done | bytes 6553632 | tf_op jit(solution)/shard_map/all_to_all | solution.py:107
  171.3 16.6 %copy.55 = bf16[20,2,640,128]{2,3,1,0:T(8,128)(2,1)} copy(bf16[20,2,640,128]{3,1,2,0:T(2,128)(2,1)} %bitcast.65) | data formatting | bytes 13107200 | tf_op jit(solution)/shard_map/all_to_all | solution.py:107
  188.0 8.3 %fusion.2 = bf16[20,2,640,128]{2,3,1,0:T(8,128)(2,1)} fusion(s32[]{:T(128)S(6)} %select_n.76, bf16[20,2,640,128]{2,3,1,0:T(8,128)(2,1)} %copy.55), kind=kLoop, calls=%fused_computation.8 | loop fusion | flops 3276800 | bytes 13107204 | tf_op jit(solution)/shard_map/jit(_roll_dynamic)/concatenate | solution.py:11
  205.9 77.5 %all_gather.3 = bf16[128,129]{1,0:T(8,128)(2,1)S(1)} all-gather(bf16[32,129]{1,0:T(8,128)(2,1)S(1)} %pad_maximum_fusion.1), channel_id=1, replica_groups=mesh['lat'=32,'lev'=4] {'lev'}, dimensions={0}, use_global_device_ids=true | all-gather | bytes 41280 | tf_op jit(solution)/shard_map/all_gather | solution.py:25
  303.6 11.6 %multiply_convert_fusion = bf16[5,640,2,512]{1,3,2,0:T(8,128)(2,1)} fusion(f32[5,640]{1,0:T(8,128)S(1)} %fusion.31, bf16[5,2,640,1024]{2,3,1,0:T(8,128)(2,1)} %slice_dynamic-update-slice_fusion.1, s32[]{:T(128)S(6)} %select_n.78, bf16[20,640,640]{2,1,0:T(8,128)(2,1)} %param.7, s32[]{:T(128)S(6)} %select_n.72), kind=kOutput, calls=%fused_computation.6 | convolution fusion | flops 4200857600 | bytes 17216008 | tf_op jit(solution)/shard_map/sna,srac->snrc/dot_general | solution.py:83
  315.2 11.8 %reshape.389 = bf16[5,640,2,128,4]{1,4,3,2,0:T(4,128)(2,1)} reshape(bf16[5,640,2,512]{1,3,2,0:T(8,128)(2,1)} %multiply_convert_fusion) | data formatting | bytes 13107200 | tf_op jit(solution)/shard_map/reshape | solution.py:117
  327.0 7.9 %fusion.1 = bf16[5,640,2,128,4]{1,3,4,2,0:T(8,128)(2,1)S(1)} fusion(bf16[5,640,2,128,4]{1,4,3,2,0:T(4,128)(2,1)} %reshape.389, f32[640,128]{0,1:T(8,128)S(1)} %add_divide_fusion, bf16[128,129]{1,0:T(8,128)(2,1)S(1)} %all_gather.3), kind=kOutput, calls=%fused_computation.5 | convolution fusion | flops 851968000 | bytes 20021248 | tf_op jit(solution)/shard_map/snrkf,lk->snrlf/dot_general | solution.py:118
  334.9 28.2 %copy.60 = bf16[5,640,2,128,4]{1,2,4,3,0:T(2,128)(2,1)S(1)} copy(bf16[5,640,2,128,4]{1,3,4,2,0:T(8,128)(2,1)S(1)} %fusion.1) | data formatting | bytes 13107200 | tf_op jit(solution)/shard_map/convert_element_type | solution.py:122
  363.1 10.1 %convert_bitcast_fusion = bf16[5,2,640,512]{2,3,1,0:T(8,128)(2,1)} fusion(bf16[5,640,2,512]{1,2,3,0:T(2,128)(2,1)S(1)} %bitcast.67, bf16[20,640,640]{2,1,0:T(8,128)(2,1)} %param.7, s32[]{:T(128)S(6)} %select_n.72), kind=kOutput, calls=%fused_computation.18 | convolution fusion | flops 4197580800 | bytes 17203204 | tf_op jit(solution)/shard_map/sna,snrc->srac/dot_general | solution.py:91
  373.2 16.7 %copy.62 = bf16[5,2,640,512]{3,1,2,0:T(2,128)(2,1)} copy(bf16[5,2,640,512]{2,3,1,0:T(8,128)(2,1)} %convert_bitcast_fusion) | data formatting | bytes 13107200 | tf_op jit(solution)/shard_map/convert_element_type | solution.py:92
  397.0 11.0 %pad_maximum_fusion = bf16[32,20,2,20,128]{4,2,3,0,1:T(2,128)(2,1)S(1)} fusion(bf16[32,5,2,20,128]{4,2,3,0,1:T(2,128)(2,1)S(1)} %get-tuple-element.6, bf16[32,5,2,20,128]{4,2,3,0,1:T(2,128)(2,1)S(1)} %get-tuple-element.7, bf16[32,5,2,20,128]{4,2,3,0,1:T(2,128)(2,1)S(1)} %get-tuple-element.8, bf16[32,5,2,20,128]{4,2,3,0,1:T(2,128)(2,1)S(1)} %get-tuple-element.5), kind=kLoop, calls=%fused_computation.9 | loop fusion | flops 9830400 | bytes 13107200 | tf_op jit(solution)/shard_map/concatenate.5
  413.9 8.8 %all-to-all-start.1 = ((bf16[128,5,2,20,128]{4,2,3,1,0:T(2,128)(2,1)}), bf16[128,5,2,20,128]{4,2,3,1,0:T(2,128)(2,1)}, u32[]{:S(2)}, u32[]{:S(2)}) async-start(bf16[128,5,2,20,128]{4,2,3,1,0:T(2,128)(2,1)} %bitcast.62), calls=%async_computation.1 | async-start | bytes 13107200 | tf_op jit(solution)/shard_map/all_to_all | solution.py:49
  422.9 15.2 %multiply_convert_fusion.3 = (bf16[640,1,1280]{2,0,1:T(8,128)(2,1)S(1)}, bf16[640,1,1280]{2,0,1:T(8,128)(2,1)S(1)}) fusion(f32[640]{0:T(1024)S(1)} %select_multiply_fusion, s32[640]{0:T(1024)S(1)} %broadcast_in_dim_reshape.4), kind=kLoop, calls=%fused_computation.37 | loop fusion | flops 11468800 | bytes 3281920 | tf_op jit(solution)/shard_map/convert.1
  438.1 63.9 %all-to-all-done.1 = bf16[128,5,2,20,128]{4,2,3,1,0:T(2,128)(2,1)} async-done(((bf16[128,5,2,20,128]{4,2,3,1,0:T(2,128)(2,1)}), bf16[128,5,2,20,128]{4,2,3,1,0:T(2,128)(2,1)}, u32[]{:S(2)}, u32[]{:S(2)}) %all-to-all-start.1) | async-done | bytes 6553632 | tf_op jit(solution)/shard_map/all_to_all | solution.py:49
  508.0 17.0 %bitcast_multiply_fusion = bf16[640,2,20,128]{3,1,2,0:T(2,128)(2,1)} fusion(bf16[32,4,5,2,20,128]{5,3,4,2,0,1:T(2,128)(2,1)S(1)} %copy.64, bf16[640,20]{1,0:T(8,128)(2,1)S(1)} %copy.66), kind=kLoop, calls=%fused_computation.10 | loop fusion | flops 3276800 | bytes 13132800 | tf_op jit(solution)/shard_map/mul | solution.py:132
  525.0 23.5 %copy.67 = bf16[20,128,640,2]{2,3,1,0:T(2,128)(2,1)} copy(bf16[20,128,640,2]{1,3,0,2:T(2,128)(2,1)} %bitcast.64) | data formatting | bytes 13107200 | tf_op jit(solution)/shard_map/mrac,mrx->acx/dot_general | solution.py:133
  548.5 13.4 %bitcast_convert_fusion = bf16[20,32,4,1280]{3,1,2,0:T(8,128)(2,1)} fusion(bf16[20,32,4,640,2]{3,4,2,1,0:T(2,128)(2,1)} %bitcast.66, bf16[640,1,1280]{2,0,1:T(8,128)(2,1)S(1)} %get-tuple-element.13, bf16[640,1,1280]{2,0,1:T(8,128)(2,1)S(1)} %get-tuple-element.12), kind=kOutput, calls=%fused_computation.2 | convolution fusion | flops 8393523200 | bytes 16384000 | tf_op jit(solution)/shard_map/mrac,mrx->acx/dot_general | solution.py:133
  561.9 11.4 %copy.69 = bf16[20,32,4,1280]{3,2,1,0:T(4,128)(2,1)} copy(bf16[20,32,4,1280]{3,1,2,0:T(8,128)(2,1)} %bitcast_convert_fusion) | data formatting | bytes 13107200 | tf_op jit(solution)/shard_map/convert_element_type | solution.py:136
  (43 shorter events, 58.6 us)
Async XLA Ops:
  77.0 87.4 %all-to-all-start = ((bf16[640,2,20,128]{3,1,2,0:T(2,128)(2,1)}), bf16[640,2,20,128]{3,1,2,0:T(2,128)(2,1)}, u32[]{:S(2)}, u32[]{:S(2)}) async-start(bf16[640,2,20,128]{3,1,2,0:T(2,128)(2,1)} %copy.53), calls=%async_computation | async-start | bytes 13107200 | tf_op jit(solution)/shard_map/all_to_all | solution.py:107
  196.3 9.5 %copy-start.1 = (bf16[32]{0:T(256)(128)(2,1)S(1)}, bf16[32]{0:T(256)(128)(2,1)}, u32[]{:S(2)}) copy-start(bf16[32]{0:T(256)(128)(2,1)} %param.9) | copy-start | bytes 196
  196.3 9.6 %copy-start = (bf16[32,128]{1,0:T(8,128)(2,1)S(1)}, bf16[32,128]{1,0:T(8,128)(2,1)}, u32[]{:S(2)}) copy-start(bf16[32,128]{1,0:T(8,128)(2,1)} %param.8) | copy-start | bytes 24580
  196.3 96.1 %slice-start = ((s8[6553600]{0:T(1024)(128)(4,1)}), s8[2359296]{0:T(1024)(128)(4,1)S(1)}, s32[]{:S(2)}) async-start(s8[6553600]{0:T(1024)(128)(4,1)} %bitcast.60), calls=%async_computation.2 | async-start | bytes 4718592
  201.2 82.5 %collective-permute-start = (bf16[5,2,640,128]{2,3,1,0:T(8,128)(2,1)}, bf16[5,2,640,128]{2,3,1,0:T(8,128)(2,1)}, u32[]{:S(2)}, u32[]{:S(2)}) collective-permute-start(bf16[5,2,640,128]{2,3,1,0:T(8,128)(2,1)} %get-tuple-element.11), channel_id=1, source_target_pairs={{0,3},{1,0},{2,1},{3,2},{4,7},{5,4},{6,5},{7,6},{8,11},{9,8},{10,9... | collective-permute-start | bytes 4915208 | tf_op jit(solution)/shard_map/ppermute | solution.py:15
  204.0 82.8 %collective-permute-start.1 = (bf16[5,2,640,128]{2,3,1,0:T(8,128)(2,1)}, bf16[5,2,640,128]{2,3,1,0:T(8,128)(2,1)}, u32[]{:S(2)}, u32[]{:S(2)}) collective-permute-start(bf16[5,2,640,128]{2,3,1,0:T(8,128)(2,1)} %get-tuple-element.10), channel_id=1, source_target_pairs={{0,2},{1,3},{2,0},{3,1},{4,6},{5,7},{6,4},{7,5},{8,10},{9,11},{10,... | collective-permute-start | bytes 4915208 | tf_op jit(solution)/shard_map/ppermute | solution.py:15
  204.4 85.2 %collective-permute-start.2 = (bf16[5,2,640,128]{2,3,1,0:T(8,128)(2,1)}, bf16[5,2,640,128]{2,3,1,0:T(8,128)(2,1)}, u32[]{:S(2)}, u32[]{:S(2)}) collective-permute-start(bf16[5,2,640,128]{2,3,1,0:T(8,128)(2,1)} %get-tuple-element.9), channel_id=1, source_target_pairs={{0,1},{1,2},{2,3},{3,0},{4,5},{5,6},{6,7},{7,4},{8,9},{9,10},{10,1... | collective-permute-start | bytes 4915208 | tf_op jit(solution)/shard_map/ppermute | solution.py:15
  283.6 8.8 %slice-start.1 = ((s8[6553600]{0:T(1024)(128)(4,1)}), s8[4194304]{0:T(1024)(128)(4,1)S(1)}, s32[]{:S(2)}) async-start(s8[6553600]{0:T(1024)(128)(4,1)} %bitcast.60), calls=%async_computation.3 | async-start | bytes 8388608
  413.9 88.1 %all-to-all-start.1 = ((bf16[128,5,2,20,128]{4,2,3,1,0:T(2,128)(2,1)}), bf16[128,5,2,20,128]{4,2,3,1,0:T(2,128)(2,1)}, u32[]{:S(2)}, u32[]{:S(2)}) async-start(bf16[128,5,2,20,128]{4,2,3,1,0:T(2,128)(2,1)} %bitcast.62), calls=%async_computation.1 | async-start | bytes 13107200 | tf_op jit(solution)/shard_map/all_to_all | solution.py:49
